TPU v7x, 32 devices: a whole 2x2x4 slice. The times are simulated.
32 devices in a mesh: row: 4 (over z), col: 8 (over y, x, core).
Axes of the slice: x: 2, y: 2, z: 4, core: 2. Of those that a mesh axis runs over, the one named last changes fastest.
Arguments:
- matrix: float32 [15360, 15360], P('row', 'col'), may hold values from -4 to 4
- rhs: float32 [15360, 4096], P('row', 'col'), may hold values from -6 to 6
- pivot_inverses: bfloat16 [2, 512, 512], replicated, may hold values from -0.046875 to 0.046875
- panel_order: int32 [2], replicated, may hold values from 0 to 29, as said below
Outputs:
- factored: bfloat16 [15360, 15360], P('row', 'col')
- updated_rhs: float32 [15360, 4096], P('row', 'col')
- rhs_norms: float32 [4096], P('col')
Inputs may be any that keep to these rules, and one draw needn't show every extreme that they name: `panel_order`: two different panel indices, one of which is the last panel, 29.
All inputs are finite; a program needn't handle non-finite values.
Results may differ from a plain program's by a relative error of at most 0.001.
Values sent between devices are 32-bit elements; how exact they have to be, the bound alone decides.
No kernel may reach another device: no remote copies, remote signals or barrier semaphores. Data moves between devices by JAX's collectives and lax.ppermute only.
A program may use at most 192 MiB of HBM per device.

v0:
```python
import jax
import jax.numpy as jnp
from jax import lax
from jax.sharding import PartitionSpec as P

N = 15360
PW = 512


def product(first, second):
    return jnp.dot(
        first, second, precision=lax.Precision.HIGHEST, preferred_element_type=jnp.float32
    )


def cut_along(values, start, length, axis_dim):
    return lax.dynamic_slice_in_dim(values, start, length, axis_dim)


def refresh(sub_block, mult_rows, upper_rows, row_keep, col_keep, fresh_col, placed):
    updated = sub_block - row_keep[:, None] * product(mult_rows, upper_rows * col_keep[None, :])
    return jnp.where((row_keep[:, None] > 0) & (fresh_col[None, :] > 0), placed, updated)


def on_device(matrix, rhs, pivot_inverses, panel_order):
    row_count = lax.axis_size("row")
    col_count = lax.axis_size("col")
    block_size = PW // row_count
    group_count = col_count // row_count
    col_index = lax.axis_index("col")
    row_len, col_len = matrix.shape
    row_block_id = jnp.arange(row_len, dtype=jnp.int32) // block_size
    col_block_id = jnp.arange(col_len, dtype=jnp.int32) // block_size

    def column_hit(panel_id):
        is_owner = col_index // row_count == panel_id % group_count
        return (
            ((col_block_id == panel_id // group_count) & is_owner).astype(jnp.float32),
            is_owner,
        )

    def take_slices(current, right_sides, panel_id):
        start = panel_id * block_size
        return (
            cut_along(current, start, block_size, 0),
            cut_along(right_sides, start, block_size, 0),
            cut_along(current, panel_id // group_count * block_size, block_size, 1),
        )

    current = matrix
    right_sides = rhs
    row_piece, rhs_piece, column_slab = take_slices(current, right_sides, panel_order[0])
    for section in range(2):
        panel_id = panel_order[section]
        row_keep = jnp.ones((row_len,), jnp.float32)
        col_keep = jnp.ones((col_len,), jnp.float32)
        for earlier in range(section + 1):
            row_keep = row_keep * (row_block_id != panel_order[earlier]).astype(jnp.float32)
            hit, owner_flag = column_hit(panel_order[earlier])
            col_keep = col_keep * (1.0 - hit)
        fresh_col, keep_is_owner = column_hit(panel_order[section])
        row_keep, col_keep, fresh_col, is_owner = (row_keep, col_keep, fresh_col, keep_is_owner)
        upper_rows, rhs_rows = (
            lax.all_gather(row_piece, "row", axis=0, tiled=True),
            lax.all_gather(rhs_piece, "row", axis=0, tiled=True),
        )
        inverse = pivot_inverses[section].astype(jnp.float32)
        own_rows = cut_along(inverse, col_index % row_count * block_size, block_size, 0)
        partial_value = jnp.where(is_owner, product(column_slab, own_rows), 0.0)
        multipliers = lax.psum(partial_value, "col")
        own_mult = cut_along(multipliers, col_index % row_count * block_size, block_size, 1)
        placed = lax.dynamic_update_slice_in_dim(
            jnp.zeros_like(current), own_mult, panel_id // group_count * block_size, 1
        )
        current = refresh(current, multipliers, upper_rows, row_keep, col_keep, fresh_col, placed)
        right_sides = right_sides - row_keep[:, None] * product(multipliers, rhs_rows)
        if section == 0:
            row_piece, rhs_piece, column_slab = take_slices(current, right_sides, panel_order[1])
    totals = lax.psum(jnp.sum(right_sides * right_sides, axis=0), "row")
    rhs_norms = jnp.sqrt(totals / N + 1e-06)
    return (current.astype(jnp.bfloat16), right_sides, rhs_norms)


def solution(mesh):
    in_specs = (P("row", "col"), P("row", "col"), P(), P())
    out_specs = (P("row", "col"), P("row", "col"), P("col"))
    return jax.shard_map(
        on_device, mesh=mesh, in_specs=in_specs, out_specs=out_specs, check_vma=False
    )
```

profile of v0, /device:TPU:0, one launch (start us, length us, event | category | flops | bytes accessed | tf_op | source)
XLA Modules:
  0.0 484.3 jit_solution(17791880367086263619)
XLA Ops:
  8.0 0.0 all-gather.9.cloned.1.call-start
  8.0 1.4 fusion.28
  10.1 1.7 constant_dynamic-slice_fusion.3
  11.8 0.0 all-gather.9.cloned.1.call-update
  11.8 0.0 all-reduce.3.cloned.1.call-start
  14.5 1.3 fusion.27
  15.7 6.9 %convolution_select_fusion.1 = f32[3840,512]{1,0:T(8,128)} fusion(pred[]{:T(512)S(6)} %eq.59, f32[3840,1920]{1,0:T(8,128)} %param.4, s32[]{:T(128)S(6)} %select_n.140, bf16[1,512,512]{2,1,0:T(8,128)(2,1)S(1)} %get-tuple-element.4, s32[]{:T(128)S(6)} %select_n.142), kind=kOutput, calls=%fused_computation.6 | convolution fusion | flops 3021864960 | bytes 9961481 | tf_op jit(solution)/shard_map/dot_general | solution.py:11
  22.6 0.0 all-reduce.3.cloned.1.call-update
  22.7 0.0 all-gather.5.cloned.1.call-start
  22.7 2.3 constant_dynamic-slice_fusion.2
  25.0 0.0 all-gather.5.cloned.1.call-update
  25.0 0.0 all-gather.11.cloned.1.call-start
  28.5 0.7 broadcast_compare_fusion
  29.2 0.7 fusion.15
  29.9 12.8 %all-gather.9.cloned.1.call-done = f32[512,512]{1,0:T(8,128)} async-done(((f32[128,512]{1,0:T(8,128)}), f32[512,512]{1,0:T(8,128)}) %all-gather.9.cloned.1.call-update) | async-done | bytes 1048592 | tf_op jit(solution)/shard_map/all_gather | solution.py:65
  42.6 103.8 %all-reduce.3.cloned.1.call-done = f32[3840,512]{1,0:T(8,128)} async-done(((f32[3840,512]{1,0:T(8,128)}), f32[3840,512]{1,0:T(8,128)}) %all-reduce.3.cloned.1.call-update) | async-done | bytes 7864336 | tf_op jit(solution)/shard_map/psum | solution.py:70
  146.4 16.6 %multiply_subtract_fusion.1 = f32[3840,512]{1,0:T(8,128)S(1)} fusion(f32[3840,512]{1,0:T(8,128)} %param.5, f32[3840,512]{1,0:T(8,128)} %all-reduce.3.cloned.1.call-done, f32[512,512]{1,0:T(8,128)} %all-gather.9.cloned.1.call-done, f32[3840]{0:T(1024)S(1)} %fusion.15), kind=kOutput, calls=%fused_computation.4 | convolution fusion | flops 12083527680 | bytes 24656896 | tf_op jit(solution)/shard_map/dot_general | solution.py:11
  163.0 0.0 copy-start
  163.0 3.2 copy-done
  166.2 0.7 constant_dynamic-slice_fusion
  167.0 0.0 all-gather.11.cloned.1.call-update
  167.0 0.2 all-reduce.5.cloned.1.call-start
  167.2 11.9 %broadcast.286.clone = f32[3840,1920]{1,0:T(8,128)} broadcast(f32[]{:T(128)} %constant.140.clone.1), dimensions={} | broadcast | bytes 29491204 | tf_op jit(solution)/shard_map/broadcast.6
  179.1 3.1 dynamic-slice_dynamic-update-slice_fusion.1
  182.2 0.0 all-gather.5.cloned.1.call-done
  182.2 61.2 %subtract_select_fusion = f32[3840,1920]{1,0:T(8,128)} fusion(f32[3840,1920]{1,0:T(8,128)} %dynamic-slice_dynamic-update-slice_fusion.1, f32[3840,1920]{1,0:T(8,128)} %param.4, f32[3840,512]{1,0:T(8,128)} %all-reduce.3.cloned.1.call-done, f32[3840]{0:T(1024)S(1)} %fusion.15, pred[1920]{0:T(1024)(128)(4,1)S(1)} %convert_compare_fusion, ...), kind=kOutput, calls=%fused_computation.1 | convolution fusion | flops 45328957440 | bytes 100298880 | tf_op jit(solution)/shard_map/dot_general | solution.py:11
  243.4 6.9 %convolution_select_fusion = f32[3840,512]{1,0:T(8,128)} fusion(pred[]{:T(512)S(6)} %eq.56, f32[3840,1920]{1,0:T(8,128)} %subtract_select_fusion, s32[]{:T(128)S(6)} %select_n.146, bf16[1,512,512]{2,1,0:T(8,128)(2,1)S(1)} %get-tuple-element.3, s32[]{:T(128)S(6)} %select_n.142), kind=kOutput, calls=%fused_computation.5 | convolution fusion | flops 3021864960 | bytes 9961481 | tf_op jit(solution)/shard_map/dot_general | solution.py:11
  250.3 0.0 all-reduce.5.cloned.1.call-update
  250.3 0.3 all-gather.7.cloned.1.call-start
  250.6 2.2 constant_dynamic-slice_fusion.1
  252.8 0.0 all-gather.7.cloned.1.call-update
  252.9 1.3 broadcast_compare_fusion.1
  254.2 1.3 fusion.14
  255.6 0.0 all-gather.11.cloned.1.call-done
  255.6 115.9 %all-reduce.5.cloned.1.call-done = f32[3840,512]{1,0:T(8,128)} async-done(((f32[3840,512]{1,0:T(8,128)}), f32[3840,512]{1,0:T(8,128)}) %all-reduce.5.cloned.1.call-update) | async-done | bytes 7864336 | tf_op jit(solution)/shard_map/psum | solution.py:70
  371.5 17.8 %multiply_reduce_fusion = (f32[512]{0:T(512)S(1)}, f32[3840,512]{1,0:T(8,128)}) fusion(f32[3840,512]{1,0:T(8,128)} %copy-done, f32[3840,512]{1,0:T(8,128)} %all-reduce.5.cloned.1.call-done, f32[512,512]{1,0:T(8,128)} %all-gather.11.cloned.1.call-done, f32[3840]{0:T(1024)S(1)} %fusion.14), kind=kOutput, calls=%fused_computation.2 | convolution fusion | flops 12087459840 | bytes 24658944 | tf_op jit(solution)/shard_map/dot_general | solution.py:11
  389.2 11.7 %psum.23 = f32[512]{0:T(512)S(1)} all-reduce(f32[512]{0:T(512)S(1)} %get-tuple-element.7), channel_id=1, replica_groups=mesh['row'=4,'col'=8] {'row'}, use_global_device_ids=true, to_apply=%region_3.4 | all-reduce | flops 512 | bytes 4096 | tf_op jit(solution)/shard_map/psum | solution.py:79
  400.9 0.6 add_sqrt_fusion
  401.5 11.6 %broadcast.286 = f32[3840,1920]{1,0:T(8,128)} broadcast(f32[]{:T(128)} %constant.140.clone.1), dimensions={} | broadcast | bytes 29491204 | tf_op jit(solution)/shard_map/broadcast.6
  413.1 3.1 dynamic-slice_dynamic-update-slice_fusion
  416.2 0.0 all-gather.7.cloned.1.call-done
  416.2 60.9 %select_convert_fusion = bf16[3840,1920]{1,0:T(8,128)(2,1)} fusion(f32[3840,1920]{1,0:T(8,128)} %dynamic-slice_dynamic-update-slice_fusion, f32[3840,1920]{1,0:T(8,128)} %subtract_select_fusion, f32[3840,512]{1,0:T(8,128)} %all-reduce.5.cloned.1.call-done, f32[3840]{0:T(1024)S(1)} %fusion.14, pred[1920]{0:T(1024)(128)(4,1)S(1)} %convert_compare_fusion.1, ...), kind=kOutput, calls=%fused_computation | convolution fusion | flops 45328957440 | bytes 85553280 | tf_op jit(solution)/shard_map/dot_general | solution.py:11
  (4 shorter events, 0.0 us)
Async XLA Ops:
  8.0 34.6 %all-gather.9.cloned.1.call-start = ((), (), s32[]{:S(2)}) async-start(), calls=%async_computation.4 | async-start | bytes 1310720 | tf_op jit(solution)/shard_map/all_gather | solution.py:65
  11.8 134.6 %all-reduce.3.cloned.1.call-start = ((), (), s32[]{:S(2)}) async-start(), calls=%async_computation | async-start | bytes 15728640 | tf_op jit(solution)/shard_map/psum | solution.py:70
  22.7 159.5 %all-gather.5.cloned.1.call-start = ((), (), s32[]{:S(2)}) async-start(), calls=%async_computation.1 | async-start | bytes 4915200 | tf_op jit(solution)/shard_map/all_gather | solution.py:64
  25.0 230.5 %all-gather.11.cloned.1.call-start = ((), (), s32[]{:S(2)}) async-start(), calls=%async_computation.5 | async-start | bytes 1310720 | tf_op jit(solution)/shard_map/all_gather | solution.py:65
  163.0 3.2 copy-start
  167.0 204.5 %all-reduce.5.cloned.1.call-start = ((), (), s32[]{:S(2)}) async-start(), calls=%async_computation.2 | async-start | bytes 15728640 | tf_op jit(solution)/shard_map/psum | solution.py:70
  250.3 165.9 %all-gather.7.cloned.1.call-start = ((), (), s32[]{:S(2)}) async-start(), calls=%async_computation.3 | async-start | bytes 4915200 | tf_op jit(solution)/shard_map/all_gather | solution.py:64
Sparse Core Ops, SparseCore 0:
  11.9 30.6 all-gather.8
  44.2 75.7 all-gather.4
  167.1 28.0 all-gather.10
  253.0 76.5 all-gather.6
Sparse Core Ops, SparseCore 1:
  22.7 123.6 all-reduce.2
  250.4 121.0 all-reduce.4
where the time goes:
time: 485 us; the launch traced here: 484 us
  waiting for transfers between devices  233 us (48%)
  matrix products  170 us (35%)
  local copies, waits for them, and re-layouts  42.5 us (9%)
  between operations  22 us (5%)
  blocking collectives  11.7 us (2%)
    psum x2, waiting for transfers between devices, on_device(): multipliers = lax.psum(partial_value, 'col')  220 us
    dot_general x6, matrix products, product(): jnp.dot(first, second, precision=lax.Precision.HIGHEST, preferred_element...  170 us
    another operation x2, local copies, waits for them, and re-layouts  23.5 us
    all_gather x2, waiting for transfers between devices, on_device(): lax.all_gather(rhs_piece, 'row', axis=0, tiled=True)  12.8 us
    psum x1, blocking collectives, on_device(): totals = lax.psum(jnp.sum(right_sides * right_sides, axis=0), 'row')  11.7 us
  transfers between devices with their start and end apart: 6, of which 3 were waited for; matrix products, arithmetic and copies ran while one was open for 31% of the time, Pallas kernels for 0%

commit v1 on v0

--- a/solution.py
+++ b/solution.py
@@ -67,7 +67,7 @@
         inverse = pivot_inverses[section].astype(jnp.float32)
         own_rows = cut_along(inverse, col_index % row_count * block_size, block_size, 0)
         partial_value = jnp.where(is_owner, product(column_slab, own_rows), 0.0)
-        multipliers = lax.psum(partial_value, "col")
+        multipliers = jnp.sum(lax.all_gather(partial_value, "col"), axis=0)
         own_mult = cut_along(multipliers, col_index % row_count * block_size, block_size, 1)
         placed = lax.dynamic_update_slice_in_dim(
             jnp.zeros_like(current), own_mult, panel_id // group_count * block_size, 1

time: 485 us -> 913 us (1.88)
  waiting for transfers between devices: 233 us -> 614 us
  other arithmetic: 4.61 us -> 52.6 us
    all_gather x0 -> x2, waiting for transfers between devices: none -> 536 us  [on_device(): multipliers = jnp.sum(lax.all_gather(partial_value, 'col'), axis=0)]
    psum x2 -> x0, waiting for transfers between devices: 220 us -> none  [on_device(): multipliers = lax.psum(partial_value, 'col')]
    all_gather x2, waiting for transfers between devices: 0.01 us -> 72.3 us  [on_device(): lax.all_gather(row_piece, 'row', axis=0, tiled=True)]
    reduce_sum x0 -> x2, other arithmetic: none -> 48.2 us  [on_device(): multipliers = jnp.sum(lax.all_gather(partial_value, 'col'), axis=0)]
  transfers between devices with their start and end apart: 6 -> 6, of which waited for: 3 -> 5; matrix products, arithmetic and copies ran while one was open for 31% -> 21% of each run, Pallas kernels for 0% -> 0%
where the time goes in v1:
time: 913 us; the launch traced here: 912 us
  waiting for transfers between devices  614 us (67%)
  matrix products  170 us (19%)
  other arithmetic  52.6 us (6%)
  local copies, waits for them, and re-layouts  43.7 us (5%)
  between operations  20.4 us (2%)
  blocking collectives  11 us (1%)
    all_gather x2, waiting for transfers between devices, on_device(): multipliers = jnp.sum(lax.all_gather(partial_value, 'col'), axis=0)  536 us
    dot_general x6, matrix products, product(): jnp.dot(first, second, precision=lax.Precision.HIGHEST, preferred_element...  170 us
    all_gather x2, waiting for transfers between devices, on_device(): lax.all_gather(row_piece, 'row', axis=0, tiled=True)  72.3 us
    reduce_sum x2, other arithmetic, on_device(): multipliers = jnp.sum(lax.all_gather(partial_value, 'col'), axis=0)  48.2 us
    another operation x2, local copies, waits for them, and re-layouts  23.5 us
  transfers between devices with their start and end apart: 6, of which 5 were waited for; matrix products, arithmetic and copies ran while one was open for 21% of the time, Pallas kernels for 0%

profile of v1, /device:TPU:0, one launch (start us, length us, event | category | flops | bytes accessed | tf_op | source)
XLA Modules:
  0.0 912.2 jit_solution(3910698292947535390)
XLA Ops:
  7.2 0.0 all-gather.17.cloned.1.call-start
  7.2 1.3 fusion.28
  11.2 1.3 fusion.27
  12.5 6.9 convolution_select_fusion.1
  19.4 0.0 all-gather.17.cloned.1.call-update
  19.4 0.0 all-gather.9.cloned.1.call-start
  20.1 2.2 constant_dynamic-slice_fusion.2
  22.3 0.0 all-gather.9.cloned.1.call-update
  22.3 0.0 all-gather.13.cloned.1.call-start
  22.4 1.7 constant_dynamic-slice_fusion.3
  24.1 0.0 all-gather.13.cloned.1.call-update
  24.1 0.2 all-gather.19.cloned.1.call-start
  24.3 0.7 fusion.15
  25.0 0.7 broadcast_compare_fusion
  27.9 279.3 %all-gather.17.cloned.1.call-done = f32[30720,512]{1,0:T(8,128)} async-done(((f32[3840,512]{1,0:T(8,128)}), f32[30720,512]{1,0:T(8,128)}) %all-gather.17.cloned.1.call-update) | async-done | bytes 62914576 | tf_op jit(solution)/shard_map/all_gather | solution.py:70
  307.2 24.5 %reduce_sum.27 = f32[3840,512]{1,0:T(8,128)} reduce(f32[8,3840,512]{2,1,0:T(8,128)} %bitcast.18, f32[]{:T(128)} %constant.140.clone.1), dimensions={0}, to_apply=%region_0.1 | reduce | flops 13762560 | bytes 70778880 | tf_op jit(solution)/shard_map/reduce_sum | solution.py:70
  331.7 11.8 %broadcast.286.clone = f32[3840,1920]{1,0:T(8,128)} broadcast(f32[]{:T(128)} %constant.140.clone.1), dimensions={} | broadcast | bytes 29491204 | tf_op jit(solution)/shard_map/broadcast.6
  343.5 3.1 dynamic-slice_dynamic-update-slice_fusion.1
  346.6 39.2 %all-gather.9.cloned.1.call-done = f32[512,1920]{1,0:T(8,128)} async-done(((f32[128,1920]{1,0:T(8,128)}), f32[512,1920]{1,0:T(8,128)}) %all-gather.9.cloned.1.call-update) | async-done | bytes 3932176 | tf_op jit(solution)/shard_map/all_gather | solution.py:64
  385.8 61.1 %subtract_select_fusion = f32[3840,1920]{1,0:T(8,128)} fusion(f32[3840,1920]{1,0:T(8,128)} %dynamic-slice_dynamic-update-slice_fusion.1, f32[3840,1920]{1,0:T(8,128)} %param.4, f32[3840,512]{1,0:T(8,128)} %reduce_sum.27, f32[3840]{0:T(1024)S(1)} %fusion.15, pred[1920]{0:T(1024)(128)(4,1)S(1)} %convert_compare_fusion, ...), kind=kOutput, calls=%fused_computation.1 | convolution fusion | flops 45328957440 | bytes 100298880 | tf_op jit(solution)/shard_map/dot_general | solution.py:11
  446.9 6.9 convolution_select_fusion
  453.8 0.0 all-gather.19.cloned.1.call-update
  453.9 0.3 all-gather.15.cloned.1.call-start
  454.7 0.0 all-gather.13.cloned.1.call-done
  454.7 16.6 %multiply_subtract_fusion.1 = f32[3840,512]{1,0:T(8,128)S(1)} fusion(f32[3840,512]{1,0:T(8,128)} %param.5, f32[3840,512]{1,0:T(8,128)} %reduce_sum.27, f32[512,512]{1,0:T(8,128)} %all-gather.13.cloned.1.call-done, f32[3840]{0:T(1024)S(1)} %fusion.15), kind=kOutput, calls=%fused_computation.4 | convolution fusion | flops 12083527680 | bytes 24656896 | tf_op jit(solution)/shard_map/dot_general | solution.py:11
  471.3 0.0 copy-start
  471.4 4.3 copy-done
  475.7 0.7 constant_dynamic-slice_fusion
  476.4 0.0 all-gather.15.cloned.1.call-update
  476.5 0.0 all-gather.11.cloned.1.call-start
  476.5 2.2 constant_dynamic-slice_fusion.1
  478.7 0.0 all-gather.11.cloned.1.call-update
  478.8 1.2 broadcast_compare_fusion.1
  480.0 1.2 fusion.14
  481.2 256.3 %all-gather.19.cloned.1.call-done = f32[30720,512]{1,0:T(8,128)} async-done(((f32[3840,512]{1,0:T(8,128)}), f32[30720,512]{1,0:T(8,128)}) %all-gather.19.cloned.1.call-update) | async-done | bytes 62914576 | tf_op jit(solution)/shard_map/all_gather | solution.py:70
  737.5 23.7 %reduce_sum.28 = f32[3840,512]{1,0:T(8,128)} reduce(f32[8,3840,512]{2,1,0:T(8,128)} %bitcast.19, f32[]{:T(128)} %constant.140.clone.1), dimensions={0}, to_apply=%region_1.2 | reduce | flops 13762560 | bytes 70778880 | tf_op jit(solution)/shard_map/reduce_sum | solution.py:70
  761.2 5.7 all-gather.15.cloned.1.call-done
  767.0 17.8 %multiply_reduce_fusion = (f32[512]{0:T(512)S(1)}, f32[3840,512]{1,0:T(8,128)}) fusion(f32[3840,512]{1,0:T(8,128)} %copy-done, f32[3840,512]{1,0:T(8,128)} %reduce_sum.28, f32[512,512]{1,0:T(8,128)} %all-gather.15.cloned.1.call-done, f32[3840]{0:T(1024)S(1)} %fusion.14), kind=kOutput, calls=%fused_computation.2 | convolution fusion | flops 12087459840 | bytes 24658944 | tf_op jit(solution)/shard_map/dot_general | solution.py:11
  784.7 11.0 %psum.7 = f32[512]{0:T(512)S(1)} all-reduce(f32[512]{0:T(512)S(1)} %get-tuple-element.7), channel_id=1, replica_groups=mesh['row'=4,'col'=8] {'row'}, use_global_device_ids=true, to_apply=%region_3.4 | all-reduce | flops 512 | bytes 4096 | tf_op jit(solution)/shard_map/psum | solution.py:79
  795.7 0.6 add_sqrt_fusion
  796.3 11.8 %broadcast.286 = f32[3840,1920]{1,0:T(8,128)} broadcast(f32[]{:T(128)} %constant.140.clone.1), dimensions={} | broadcast | bytes 29491204 | tf_op jit(solution)/shard_map/broadcast.6
  808.0 3.2 dynamic-slice_dynamic-update-slice_fusion
  811.3 33.1 %all-gather.11.cloned.1.call-done = f32[512,1920]{1,0:T(8,128)} async-done(((f32[128,1920]{1,0:T(8,128)}), f32[512,1920]{1,0:T(8,128)}) %all-gather.11.cloned.1.call-update) | async-done | bytes 3932176 | tf_op jit(solution)/shard_map/all_gather | solution.py:64
  844.4 60.9 %select_convert_fusion = bf16[3840,1920]{1,0:T(8,128)(2,1)} fusion(f32[3840,1920]{1,0:T(8,128)} %dynamic-slice_dynamic-update-slice_fusion, f32[3840,1920]{1,0:T(8,128)} %subtract_select_fusion, f32[3840,512]{1,0:T(8,128)} %reduce_sum.28, f32[3840]{0:T(1024)S(1)} %fusion.14, pred[1920]{0:T(1024)(128)(4,1)S(1)} %convert_compare_fusion.1, ...), kind=kOutput, calls=%fused_computation | convolution fusion | flops 45328957440 | bytes 85553280 | tf_op jit(solution)/shard_map/dot_general | solution.py:11
  (4 shorter events, 0.0 us)
Async XLA Ops:
  7.2 300.1 %all-gather.17.cloned.1.call-start = ((), (), s32[]{:S(2)}) async-start(), calls=%async_computation.4 | async-start | bytes 70778880 | tf_op jit(solution)/shard_map/all_gather | solution.py:70
  19.4 366.4 %all-gather.9.cloned.1.call-start = ((), (), s32[]{:S(2)}) async-start(), calls=%async_computation | async-start | bytes 4915200 | tf_op jit(solution)/shard_map/all_gather | solution.py:64
  22.3 432.4 %all-gather.13.cloned.1.call-start = ((), (), s32[]{:S(2)}) async-start(), calls=%async_computation.2 | async-start | bytes 1310720 | tf_op jit(solution)/shard_map/all_gather | solution.py:65
  24.1 713.4 %all-gather.19.cloned.1.call-start = ((), (), s32[]{:S(2)}) async-start(), calls=%async_computation.5 | async-start | bytes 70778880 | tf_op jit(solution)/shard_map/all_gather | solution.py:70
  453.9 313.1 %all-gather.15.cloned.1.call-start = ((), (), s32[]{:S(2)}) async-start(), calls=%async_computation.3 | async-start | bytes 1310720 | tf_op jit(solution)/shard_map/all_gather | solution.py:65
  471.3 4.4 copy-start
  476.5 368.0 %all-gather.11.cloned.1.call-start = ((), (), s32[]{:S(2)}) async-start(), calls=%async_computation.1 | async-start | bytes 4915200 | tf_op jit(solution)/shard_map/all_gather | solution.py:64
Sparse Core Ops, SparseCore 0:
  19.5 287.6 all-gather.16
  309.4 76.4 all-gather.8
  387.4 26.4 all-gather.12
  454.0 283.4 all-gather.18
  738.9 27.9 all-gather.14
  768.4 75.9 all-gather.10
